TPU v7x, 32 devices: a whole 2x2x4 slice. The times are simulated.
32 devices in a mesh: seq: 8 (over z, y), tp: 4 (over x, core).
Axes of the slice: x: 2, y: 2, z: 4, core: 2. Of those that a mesh axis runs over, the one named last changes fastest.
Arguments:
- inputs: bfloat16 [2, 32, 8192], P(None, 'seq', 'tp'), may hold values from -6 to 6
- out_grad: bfloat16 [2, 32, 8192], P(None, 'seq', 'tp'), may hold values from -6 to 6
- gate_weight: bfloat16 [8192, 14848], P('tp', 'seq'), may hold values from -0.0625 to 0.0625
- up_weight: bfloat16 [8192, 14848], P('tp', 'seq'), may hold values from -0.0625 to 0.0625
- down_weight: bfloat16 [14848, 8192], P('seq', 'tp'), may hold values from -0.0625 to 0.0625
Outputs:
- input_grad: bfloat16 [2, 32, 8192], P(None, 'seq', 'tp')
- gate_grad: float32 [8192, 14848], P('tp', 'seq')
- up_grad: float32 [8192, 14848], P('tp', 'seq')
- down_grad: float32 [14848, 8192], P('seq', 'tp')
All inputs are finite; a program needn't handle non-finite values.
Results may differ from a plain program's by a relative error of at most 0.0049.
Values may be sent and summed in bfloat16 or wider, within the bound.
A program may use at most 128 MiB of HBM per device.

v0:
```python
import jax
import jax.numpy as jnp
from jax import lax
from jax.sharding import PartitionSpec as P


def per_device(inputs, out_grad, gate_weight, up_weight, down_weight):
    blocks = inputs.shape[0]
    local_rows = inputs.shape[1]
    width_count = lax.axis_size("tp")
    block_tokens = local_rows * lax.axis_size("seq")
    share_rows = block_tokens // width_count
    share_start = lax.axis_index("tp") * share_rows
    contract_first = (((0,), (0,)), ((), ()))
    contract_last = (((1,), (1,)), ((), ()))
    totals = None
    results = [None] * blocks
    for index in range(blocks):
        whole_in = lax.all_gather(inputs[index], "seq", axis=0, tiled=True)
        whole_grad = lax.all_gather(out_grad[index], "seq", axis=0, tiled=True)
        gate_part = jnp.dot(whole_in, gate_weight, preferred_element_type=jnp.float32)
        up_part = jnp.dot(whole_in, up_weight, preferred_element_type=jnp.float32)
        gate, up_proj = lax.psum((gate_part, up_part), "tp")
        hidden_share = lax.psum_scatter(
            lax.dot_general(
                whole_grad, down_weight, contract_last, preferred_element_type=jnp.float32
            ),
            "tp",
            scatter_dimension=0,
            tiled=True,
        )
        gate_share = lax.dynamic_slice_in_dim(gate, share_start, share_rows, 0)
        up_share = lax.dynamic_slice_in_dim(up_proj, share_start, share_rows, 0)
        sig = jax.nn.sigmoid(gate_share)
        up_local = (hidden_share * gate_share * sig).astype(jnp.bfloat16)
        gate_local = (hidden_share * up_share * sig * (1.0 + gate_share * (1.0 - sig))).astype(
            jnp.bfloat16
        )
        front_unit_gate = lax.all_gather(gate_local, "tp", axis=0, tiled=True)
        front_unit_up = lax.all_gather(up_local, "tp", axis=0, tiled=True)
        hidden = (jax.nn.silu(gate) * up_proj).astype(jnp.bfloat16)
        down_term = lax.dot_general(
            hidden, whole_grad, contract_first, preferred_element_type=jnp.float32
        )
        gate_term = lax.dot_general(
            whole_in, front_unit_gate, contract_first, preferred_element_type=jnp.float32
        )
        up_term = lax.dot_general(
            whole_in, front_unit_up, contract_first, preferred_element_type=jnp.float32
        )
        terms = (gate_term, up_term, down_term)
        if totals is None:
            totals = terms
        else:
            totals = (totals[0] + terms[0], totals[1] + terms[1], totals[2] + terms[2])
        first = lax.dot_general(
            front_unit_gate, gate_weight, contract_last, preferred_element_type=jnp.float32
        )
        second = lax.dot_general(
            front_unit_up, up_weight, contract_last, preferred_element_type=jnp.float32
        )
        results[index] = lax.psum_scatter(
            first + second, "seq", scatter_dimension=0, tiled=True
        ).astype(jnp.bfloat16)
    return (jnp.stack(results), totals[0], totals[1], totals[2])


def solution(mesh):
    return jax.shard_map(
        per_device,
        mesh=mesh,
        in_specs=(
            P(None, "seq", "tp"),
            P(None, "seq", "tp"),
            P("tp", "seq"),
            P("tp", "seq"),
            P("seq", "tp"),
        ),
        out_specs=(P(None, "seq", "tp"), P("tp", "seq"), P("tp", "seq"), P("seq", "tp")),
        check_vma=False,
    )
```

profile of v0, /device:TPU:0, one launch (start us, length us, event | category | flops | bytes accessed | tf_op | source)
XLA Modules:
  0.0 335.3 jit_solution(6774601214005411477)
XLA Ops:
  7.2 0.0 all-reduce.9.cloned.1.call-start
  7.2 0.0 copy-start
  7.2 0.9 fusion.32
  8.2 32.8 %all-gather.3 = bf16[1,32,2048]{2,0,1:T(2,128)(2,1)S(1)} all-gather(bf16[1,4,2048]{2,0,1:T(2,128)(2,1)S(1)} %copy.24), channel_id=5, replica_groups=mesh['seq'=8,'tp'=4] {'seq'}, dimensions={1}, use_global_device_ids=true | all-gather | bytes 147456 | tf_op jit(solution)/shard_map/all_gather | solution.py:19
  41.0 0.1 copy.20
  41.1 30.7 %all-gather.1 = bf16[1,32,2048]{2,0,1:T(2,128)(2,1)S(1)} all-gather(bf16[1,4,2048]{2,0,1:T(2,128)(2,1)S(1)} %copy.22), channel_id=3, replica_groups=mesh['seq'=8,'tp'=4] {'seq'}, dimensions={1}, use_global_device_ids=true | all-gather | bytes 147456 | tf_op jit(solution)/shard_map/all_gather | solution.py:19
  71.8 0.1 copy.18
  71.9 0.0 copy-start.1
  71.9 0.0 slice-start
  71.9 6.4 %fusion.13 = f32[32,1856]{1,0:T(8,128)} fusion(bf16[2048,1856]{0,1:T(8,128)(2,1)} %param.7, bf16[1,32,2048]{2,1,0:T(8,128)(2,1)S(1)} %copy.18), kind=kOutput, calls=%fused_computation.20 | convolution fusion | flops 243269632 | bytes 7970816 | tf_op jit(solution)/shard_map/dot_general | solution.py:21
  78.3 0.0 copy-done.1
  78.3 0.0 copy-done
  78.3 3.0 fusion.15
  81.3 0.0 slice-done
  81.3 0.0 slice-done.1
  81.3 0.0 slice-start.6
  81.4 3.0 fusion.2
  84.4 3.0 fusion.4
  87.4 0.0 copy-done.8
  87.5 30.7 %all-gather.2 = bf16[1,32,2048]{2,0,1:T(2,128)(2,1)S(1)} all-gather(bf16[1,4,2048]{2,0,1:T(2,128)(2,1)S(1)} %copy.23), channel_id=4, replica_groups=mesh['seq'=8,'tp'=4] {'seq'}, dimensions={1}, use_global_device_ids=true | all-gather | bytes 147456 | tf_op jit(solution)/shard_map/all_gather | solution.py:20
  118.3 32.9 %all-gather = bf16[1,32,2048]{2,0,1:T(2,128)(2,1)} all-gather(bf16[1,4,2048]{2,0,1:T(2,128)(2,1)S(1)} %copy.21), channel_id=2, replica_groups=mesh['seq'=8,'tp'=4] {'seq'}, dimensions={1}, use_global_device_ids=true | all-gather | bytes 147456 | tf_op jit(solution)/shard_map/all_gather | solution.py:20
  151.2 0.0 slice-done.6
  151.2 0.0 slice-done.7
  151.2 0.0 copy-start.10
  151.2 0.0 copy-start.9
  151.2 4.0 %fusion.19 = f32[32,1856]{1,0:T(8,128)} fusion(bf16[1856,2048]{1,0:T(8,128)(2,1)S(1)} %bitcast.63, bf16[1,32,2048]{2,0,1:T(2,128)(2,1)} %all-gather), kind=kOutput, calls=%fused_computation.26 | convolution fusion | flops 243269632 | bytes 7970816 | tf_op jit(solution)/shard_map/dot_general | solution.py:25
  155.2 0.0 copy-done.3
  155.2 3.0 fusion.7
  158.3 0.0 all-reduce.9.cloned.1.call-update
  158.3 0.0 copy-done.10
  158.3 0.6 dynamic-slice.2
  159.0 0.0 copy-done.9
  159.0 0.6 dynamic-slice
  160.8 40.2 %all-reduce.9.cloned.1.call-done = (f32[32,1856]{1,0:T(8,128)}, f32[32,1856]{1,0:T(8,128)}, f32[32,1856]{1,0:T(8,128)}, f32[32,1856]{1,0:T(8,128)}, f32[32,1856]{1,0:T(8,128)}, /*index=5*/f32[32,1856]{1,0:T(8,128)}) async-done(((f32[32,1856]{1,0:T(8,128)}, f32[32,1856]{1,0:T(8,128)}, f32[32,1856]{1,0:T(8,128)}, f32[32,1856]{1,0:T(8,128)}, f32[32,1856]{1,0:T(8,128)}, /*index=5*/f32[32,1856]{1,0:T(8,128)}), ...) | async-done | bytes 1425424 | tf_op jit(solution)/shard_map/psum | solution.py:23
  201.0 3.5 %fusion.17 = f32[1856,2048]{1,0:T(8,128)S(1)} fusion(f32[32,1856]{1,0:T(8,128)} %get-tuple-element.9, f32[32,1856]{1,0:T(8,128)} %get-tuple-element.11, bf16[1,32,2048]{2,0,1:T(2,128)(2,1)} %all-gather), kind=kOutput, calls=%fused_computation.24 | convolution fusion | flops 243625984 | bytes 15810560 | tf_op jit(solution)/shard_map/dot_general | solution.py:42
  204.5 0.9 multiply_convert_fusion.6
  205.5 5.4 %all_gather.26 = bf16[32,1856]{1,0:T(8,128)(2,1)S(1)} all-gather(bf16[8,1856]{1,0:T(8,128)(2,1)S(1)} %get-tuple-element.13), channel_id=1, replica_groups=mesh['seq'=8,'tp'=4] {'tp'}, dimensions={0}, use_global_device_ids=true | all-gather | bytes 148480 | tf_op jit(solution)/shard_map/all_gather | solution.py:39
  210.9 0.0 slice-done.2
  210.9 0.0 slice-done.3
  210.9 1.4 fusion.33
  212.3 0.0 copy-done.2
  212.3 0.0 copy-start.6
  212.3 0.0 copy-start.7
  212.3 0.0 slice-start.4
  212.3 7.8 %fusion.11 = f32[1856,2048]{1,0:T(8,128)} fusion(bf16[32,1856]{1,0:T(8,128)(2,1)S(1)} %all_gather.26, bf16[1,32,2048]{2,1,0:T(8,128)(2,1)S(1)} %copy-done.2), kind=kOutput, calls=%fused_computation.18 | convolution fusion | flops 243269632 | bytes 15454208 | tf_op jit(solution)/shard_map/dot_general | solution.py:45
  220.1 0.0 copy-done.6
  220.1 0.0 copy-done.7
  220.1 0.9 multiply_convert_fusion.4
  221.0 0.0 slice-start.5
  221.0 5.5 %all_gather.31 = bf16[32,1856]{1,0:T(8,128)(2,1)S(1)} all-gather(bf16[8,1856]{1,0:T(8,128)(2,1)S(1)} %get-tuple-element.14), channel_id=1, replica_groups=mesh['seq'=8,'tp'=4] {'tp'}, dimensions={0}, use_global_device_ids=true | all-gather | bytes 148480 | tf_op jit(solution)/shard_map/all_gather | solution.py:40
  226.5 5.4 %all_gather.27 = bf16[32,1856]{1,0:T(8,128)(2,1)S(1)} all-gather(bf16[8,1856]{1,0:T(8,128)(2,1)S(1)} %get-tuple-element.12), channel_id=1, replica_groups=mesh['seq'=8,'tp'=4] {'tp'}, dimensions={0}, use_global_device_ids=true | all-gather | bytes 148480 | tf_op jit(solution)/shard_map/all_gather | solution.py:40
  231.9 5.6 %all_gather.30 = bf16[32,1856]{1,0:T(8,128)(2,1)S(1)} all-gather(bf16[8,1856]{1,0:T(8,128)(2,1)S(1)} %get-tuple-element.15), channel_id=1, replica_groups=mesh['seq'=8,'tp'=4] {'tp'}, dimensions={0}, use_global_device_ids=true | all-gather | bytes 148480 | tf_op jit(solution)/shard_map/all_gather | solution.py:39
  237.5 7.8 %fusion.9 = f32[1856,2048]{1,0:T(8,128)} fusion(bf16[32,1856]{1,0:T(8,128)(2,1)S(1)} %all_gather.27, bf16[1,32,2048]{2,1,0:T(8,128)(2,1)S(1)} %copy-done.2), kind=kOutput, calls=%fused_computation.16 | convolution fusion | flops 243269632 | bytes 15454208 | tf_op jit(solution)/shard_map/dot_general | solution.py:48
  245.3 0.0 slice-done.4
  245.3 2.1 convolution_add_fusion.2
  247.5 1.4 fusion.34
  248.9 1.4 convolution_add_fusion.1
  250.3 0.0 copy-done.4
  250.3 7.8 %convolution_add_fusion = f32[1856,2048]{1,0:T(8,128)} fusion(f32[1856,2048]{1,0:T(8,128)S(1)} %fusion.17, f32[32,1856]{1,0:T(8,128)S(1)} %copy-done.6, f32[32,1856]{1,0:T(8,128)S(1)} %copy-done.7, bf16[1,32,2048]{2,0,1:T(2,128)(2,1)S(1)} %copy-done.4), kind=kOutput, calls=%fused_computation.2 | convolution fusion | flops 247427072 | bytes 31014912 | tf_op jit(solution)/shard_map/dot_general | solution.py:42
  258.2 13.1 %add_bitcast_fusion = f32[2048,1856]{0,1:T(8,128)} fusion(f32[1856,2048]{1,0:T(8,128)} %fusion.9, bf16[32,1856]{1,0:T(8,128)(2,1)S(1)} %all_gather.31, bf16[1,32,2048]{2,1,0:T(8,128)(2,1)S(1)} %copy.20), kind=kOutput, calls=%fused_computation | convolution fusion | flops 247070720 | bytes 30658560 | tf_op jit(solution)/shard_map/dot_general | solution.py:48
  271.3 13.2 %add_bitcast_fusion.1 = f32[2048,1856]{0,1:T(8,128)} fusion(f32[1856,2048]{1,0:T(8,128)} %fusion.11, bf16[32,1856]{1,0:T(8,128)(2,1)S(1)} %all_gather.30, bf16[1,32,2048]{2,1,0:T(8,128)(2,1)S(1)} %copy.20), kind=kOutput, calls=%fused_computation.1 | convolution fusion | flops 247070720 | bytes 30658560 | tf_op jit(solution)/shard_map/dot_general | solution.py:45
  284.5 0.0 copy-done.5
  284.5 43.3 %all-reduce.10 = (bf16[32,2048]{1,0:T(8,128)(2,1)S(1)}, bf16[32,2048]{1,0:T(8,128)(2,1)S(1)}) all-reduce(f32[32,2048]{1,0:T(8,128)S(1)} %convolution_add_fusion.1, f32[32,2048]{1,0:T(8,128)S(1)} %copy-done.5), channel_id=9, replica_groups=mesh['seq'=8,'tp'=4] {'seq'}, use_global_device_ids=true, to_apply=%region_7.8.clone | all-reduce | flops 131072 | bytes 786432
  327.8 0.6 pad_maximum_fusion
  (20 shorter events, 0.2 us)
Async XLA Ops:
  7.2 193.8 %all-reduce.9.cloned.1.call-start = ((), (), s32[]{:S(2)}) async-start(), calls=%async_computation | async-start | bytes 2949120 | tf_op jit(solution)/shard_map/psum | solution.py:23
  7.2 71.1 %copy-start = (bf16[2048,1856]{0,1:T(8,128)(2,1)S(1)}, bf16[2048,1856]{0,1:T(8,128)(2,1)}, u32[]{:S(2)}) copy-start(bf16[2048,1856]{0,1:T(8,128)(2,1)} %param.8) | copy-start | bytes 22806532
  71.9 6.4 %copy-start.1 = (bf16[1,32,2048]{2,1,0:T(8,128)(2,1)}, bf16[1,32,2048]{2,1,0:T(8,128)(2,1)S(1)}, u32[]{:S(2)}) copy-start(bf16[1,32,2048]{2,1,0:T(8,128)(2,1)S(1)} %copy.18) | copy-start | bytes 393220
  71.9 9.4 %slice-start = ((s8[7602176]{0:T(1024)(128)(4,1)}), s8[4194304]{0:T(1024)(128)(4,1)S(1)}, s32[]{:S(2)}) async-start(s8[7602176]{0:T(1024)(128)(4,1)} %bitcast.56), calls=%async_computation.1 | async-start | bytes 8388608
  78.3 3.0 slice-start.1
  81.3 6.1 %copy-start.8 = (bf16[2,4,2048]{2,1,0:T(4,128)(2,1)S(1)}, bf16[2,4,2048]{2,1,0:T(4,128)(2,1)}, u32[]{:S(2)}) copy-start(bf16[2,4,2048]{2,1,0:T(4,128)(2,1)} %param.6) | copy-start | bytes 98308
  81.3 69.8 %slice-start.6 = ((s8[7602176]{0:T(1024)(128)(4,1)}), s8[4194304]{0:T(1024)(128)(4,1)S(1)}, s32[]{:S(2)}) async-start(s8[7602176]{0:T(1024)(128)(4,1)} %bitcast.62), calls=%async_computation.7 | async-start | bytes 8388608
  84.4 66.8 %slice-start.7 = ((s8[7602176]{0:T(1024)(128)(4,1)}), s8[3407872]{0:T(1024)(128)(4,1)S(1)}, s32[]{:S(2)}) async-start(s8[7602176]{0:T(1024)(128)(4,1)} %bitcast.62), calls=%async_computation.8 | async-start | bytes 6815744
  118.3 37.0 %copy-start.3 = (bf16[1,32,2048]{2,0,1:T(2,128)(2,1)}, bf16[1,32,2048]{2,0,1:T(2,128)(2,1)S(1)}, u32[]{:S(2)}) copy-start(bf16[1,32,2048]{2,0,1:T(2,128)(2,1)S(1)} %all-gather.2) | copy-start | bytes 393220
  151.2 7.1 %copy-start.10 = (u32[32]{0:T(128)S(1)}, u32[32]{0:T(128)}, u32[]{:S(2)}) copy-start(u32[32]{0:T(128)} %constant.23) | copy-start | bytes 388
  151.2 7.8 %copy-start.9 = (u32[32]{0:T(128)S(1)}, u32[32]{0:T(128)}, u32[]{:S(2)}) copy-start(u32[32]{0:T(128)} %constant.19) | copy-start | bytes 388
  158.3 52.6 %slice-start.2 = ((s8[7602176]{0:T(1024)(128)(4,1)}), s8[3407872]{0:T(1024)(128)(4,1)S(1)}, s32[]{:S(2)}) async-start(s8[7602176]{0:T(1024)(128)(4,1)} %bitcast.58), calls=%async_computation.3 | async-start | bytes 6815744
  201.0 9.9 %slice-start.3 = ((s8[7602176]{0:T(1024)(128)(4,1)}), s8[4194304]{0:T(1024)(128)(4,1)S(1)}, s32[]{:S(2)}) async-start(s8[7602176]{0:T(1024)(128)(4,1)} %bitcast.58), calls=%async_computation.4 | async-start | bytes 8388608
  210.9 1.4 copy-start.2
  212.3 7.8 %copy-start.6 = (f32[32,1856]{1,0:T(8,128)S(1)}, f32[32,1856]{1,0:T(8,128)}, u32[]{:S(2)}) copy-start(f32[32,1856]{1,0:T(8,128)} %get-tuple-element.6) | copy-start | bytes 712708
  212.3 7.8 %copy-start.7 = (f32[32,1856]{1,0:T(8,128)S(1)}, f32[32,1856]{1,0:T(8,128)}, u32[]{:S(2)}) copy-start(f32[32,1856]{1,0:T(8,128)} %get-tuple-element.8) | copy-start | bytes 712708
  212.3 33.0 %slice-start.4 = ((s8[7602176]{0:T(1024)(128)(4,1)}), s8[4194304]{0:T(1024)(128)(4,1)S(1)}, s32[]{:S(2)}) async-start(s8[7602176]{0:T(1024)(128)(4,1)} %bitcast.60), calls=%async_computation.5 | async-start | bytes 8388608
  221.0 24.3 %slice-start.5 = ((s8[7602176]{0:T(1024)(128)(4,1)}), s8[3407872]{0:T(1024)(128)(4,1)S(1)}, s32[]{:S(2)}) async-start(s8[7602176]{0:T(1024)(128)(4,1)} %bitcast.60), calls=%async_computation.6 | async-start | bytes 6815744
  248.9 1.5 copy-start.4
  271.3 13.2 %copy-start.5 = (f32[32,2048]{1,0:T(8,128)S(1)}, f32[32,2048]{1,0:T(8,128)}, u32[]{:S(2)}) copy-start(f32[32,2048]{1,0:T(8,128)} %convolution_add_fusion.2) | copy-start | bytes 786436
Sparse Core Ops, SparseCore 0:
  158.4 42.5 all-reduce.8
where the time goes:
time: 336 us; the launch traced here: 335 us
  blocking collectives  192 us (57%)
  matrix products  82.2 us (24%)
  waiting for transfers between devices  40.2 us (12%)
  between operations  15.5 us (5%)
    all_gather x2, blocking collectives, per_device(): whole_grad = lax.all_gather(out_grad[index], 'seq', axis=0, tiled=True)  63.7 us
    all_gather x2, blocking collectives, per_device(): whole_in = lax.all_gather(inputs[index], 'seq', axis=0, tiled=True)  63.6 us
    unnamed x1, blocking collectives  43.3 us
    psum x1, waiting for transfers between devices, per_device(): gate, up_proj = lax.psum((gate_part, up_part), 'tp')  40.2 us
    dot_general x2, matrix products, per_device(): lax.dot_general(whole_in, front_unit_gate, contract_first, preferred_elem...  21 us
    dot_general x2, matrix products, per_device(): lax.dot_general(whole_in, front_unit_up, contract_first, preferred_elemen...  20.9 us
    dot_general x2, matrix products, per_device(): lax.dot_general(hidden, whole_grad, contract_first, preferred_element_typ...  11.4 us
    all_gather x2, blocking collectives, per_device(): front_unit_gate = lax.all_gather(gate_local, 'tp', axis=0, tiled=True)  11 us
  transfers between devices with their start and end apart: 1, of which 1 were waited for; matrix products, arithmetic and copies ran while one was open for 0% of the time, Pallas kernels for 0%

commit v1 on v0

v1 whole, which is shorter than its diff:
```python
import functools

import jax
import jax.numpy as jnp
from jax import lax
from jax.experimental import pallas as pl
from jax.experimental.pallas import tpu as pltpu
from jax.sharding import PartitionSpec as P

MESH = pl.DeviceIdType.MESH
F32 = jnp.float32
BF16 = jnp.bfloat16
NT = (((1,), (1,)), ((), ()))
TILE = 256
ROWS = 128


def tiles_of(size, tile, body):
    whole = size // tile

    @pl.loop(0, whole)
    def _(i):
        body(pl.multiple_of(i * tile, tile), tile)

    if size % tile:
        body(whole * tile, size % tile)


def front_kernel(n_seq, n_tp, x_ref, dy_ref, wg_hbm, wu_hbm, wd_hbm,
                 x_out, dy_out, hid_out, gu_out, uu_out, ig_out,
                 gath, wg, wu, wd, part, from_core, chip_sum, sendx, from_chip, acts,
                 w_sem, z_send, z_recv, y_send, y_recv,
                 c_send, c_recv, r_send, r_recv, a_send, a_recv, f_send, f_recv):
    seq = lax.axis_index("seq")
    tp = lax.axis_index("tp")
    nz, nchip = n_seq // 2, n_tp // 2
    z, y = seq // 2, lax.rem(seq, 2)
    chip, core = tp // 2, lax.rem(tp, 2)
    tokens, ffw = hid_out.shape
    share = tokens // n_tp
    at_y = {"seq": z * 2 + (1 - y)}
    at_core = {"tp": chip * 2 + (1 - core)}

    def z_at(k):
        return lax.rem(z + k, nz)

    def chip_at(k):
        return lax.rem(chip + k, nchip)

    loads = [
        pltpu.make_async_copy(src, dst, w_sem.at[i])
        for i, (src, dst) in enumerate(((wg_hbm, wg), (wu_hbm, wu), (wd_hbm, wd)))
    ]
    for load in loads:
        load.start()

    barrier = pltpu.get_barrier_semaphore()
    for k in range(1, nz):
        pl.semaphore_signal(barrier, inc=1, device_id={"seq": z_at(k) * 2 + y}, device_id_type=MESH)
    for k in range(1, nchip):
        pl.semaphore_signal(barrier, inc=1, device_id={"tp": chip_at(k) * 2 + core}, device_id_type=MESH)
    pl.semaphore_signal(barrier, inc=1, device_id=at_y, device_id_type=MESH)
    pl.semaphore_signal(barrier, inc=1, device_id=at_core, device_id_type=MESH)
    pl.semaphore_wait(barrier, nz - 1 + nchip - 1 + 2)

    def remote(src, dst, send, recv, to):
        return pltpu.make_async_remote_copy(
            src_ref=src, dst_ref=dst, send_sem=send, recv_sem=recv, device_id=to, device_id_type=MESH
        )

    z_copies, y_copies = [], []
    for a, ref in enumerate((x_ref, dy_ref)):
        own = [
            remote(ref, gath.at[a, z, y], z_send.at[a, k], z_recv.at[a, k], {"seq": z_at(k) * 2 + y})
            for k in range(1, nz)
        ]
        over = [remote(ref, gath.at[a, z, y], y_send.at[a, 0], y_recv.at[a, 0], at_y)]
        over += [
            remote(gath.at[a, z_at(nz - k), y], gath.at[a, z_at(nz - k), y],
                   y_send.at[a, k], y_recv.at[a, k], at_y)
            for k in range(1, nz)
        ]
        z_copies.append(own)
        y_copies.append(over)
    for a in range(2):
        y_copies[a][0].start()
        for copy in z_copies[a]:
            copy.start()
    for a, ref in enumerate((x_ref, dy_ref)):
        gath[a, z, y] = ref[...]

    def forward(a):
        for k in range(1, nz):
            z_copies[a][k - 1].wait_recv()
            y_copies[a][k].start()

    def arrive(a, out):
        for k in range(nz):
            y_copies[a][k].wait_recv()
        out[...] = gath[a].astype(F32).reshape(out.shape).astype(BF16)

    c_copies = [
        remote(part.at[q, :, 1 - core], from_core.at[q], c_send.at[q], c_recv.at[q], at_core)
        for q in range(3)
    ]
    r_copies = [
        [
            remote(sendx.at[q, k - 1], from_chip.at[q, k - 1], r_send.at[q, k], r_recv.at[q, k],
                   {"tp": chip_at(k) * 2 + core})
            for k in range(1, nchip)
        ]
        for q in range(3)
    ]

    def product(q, out, w, last):
        def body(start, width):
            if last:
                val = lax.dot_general(out[...], w[pl.ds(start, width), :], NT, preferred_element_type=F32)
            else:
                val = jnp.dot(out[...], w[:, pl.ds(start, width)], preferred_element_type=F32)
            part[q, :, :, :, pl.ds(start, width)] = val.reshape(nchip, 2, share, width)

        tiles_of(ffw, TILE, body)
        c_copies[q].start()

    def reduce_chip(q):
        c_copies[q].wait_recv()
        for k in range(1, nchip):
            sendx[q, k - 1] = (part[q, chip_at(k), core] + from_core[q, chip_at(k)]).astype(BF16)
            r_copies[q][k - 1].start()
        chip_sum[q] = part[q, chip, core] + from_core[q, chip]

    forward(0)
    arrive(0, x_out)
    loads[0].wait()
    product(0, x_out, wg, False)
    forward(1)
    loads[1].wait()
    product(1, x_out, wu, False)
    reduce_chip(0)
    reduce_chip(1)
    arrive(1, dy_out)
    loads[2].wait()
    product(2, dy_out, wd, True)
    reduce_chip(2)
    for q in range(3):
        for k in range(1, nchip):
            r_copies[q][k - 1].wait_recv()

    def total(q):
        value = chip_sum[q]
        for k in range(1, nchip):
            value = value + from_chip[q, k - 1].astype(F32)
        return value

    gate, up, grad = total(0), total(1), total(2)
    sig = jax.nn.sigmoid(gate)
    acts[0, chip, core] = (grad * up * sig * (1.0 + gate * (1.0 - sig))).astype(BF16)
    acts[1, chip, core] = (grad * gate * sig).astype(BF16)
    acts[2, chip, core] = (gate * sig * up).astype(BF16)

    a_copies, f_copies = [], []
    for q in range(3):
        mine = acts.at[q, chip, core]
        a_copies.append([
            remote(mine, mine, a_send.at[q, k], a_recv.at[q, k], {"tp": chip_at(k) * 2 + core})
            for k in range(1, nchip)
        ])
        over = [remote(mine, mine, f_send.at[q, 0], f_recv.at[q, 0], at_core)]
        for k in range(1, nchip):
            theirs = acts.at[q, chip_at(nchip - k), core]
            over.append(remote(theirs, theirs, f_send.at[q, k], f_recv.at[q, k], at_core))
        f_copies.append(over)
    for q in range(3):
        for copy in a_copies[q]:
            copy.start()
        f_copies[q][0].start()
    outs = (gu_out, uu_out, hid_out)

    def settle(q):
        for k in range(1, nchip):
            a_copies[q][k - 1].wait_recv()
            f_copies[q][k].start()

    def collect(q):
        for k in range(nchip):
            f_copies[q][k].wait_recv()
        outs[q][...] = acts[q].reshape(tokens, ffw)

    def back(q, w):
        def body(start, width):
            val = lax.dot_general(outs[q][...], w[pl.ds(start, width), :], NT, preferred_element_type=F32)
            if q:
                val = val + ig_out[:, pl.ds(start, width)]
            ig_out[:, pl.ds(start, width)] = val

        tiles_of(ig_out.shape[1], TILE, body)

    settle(0)
    settle(1)
    collect(0)
    back(0, wg)
    settle(2)
    collect(1)
    back(1, wu)
    collect(2)

    for a in range(2):
        for copy in z_copies[a] + y_copies[a]:
            copy.wait_send()
    for q in range(3):
        for copy in [c_copies[q]] + r_copies[q] + a_copies[q] + f_copies[q]:
            copy.wait_send()


def front(n_seq, n_tp, x, dy, wg, wu, wd):
    rows, width = x.shape
    ffw = wg.shape[1]
    tokens = rows * n_seq
    nz, nchip = n_seq // 2, n_tp // 2
    share = tokens // n_tp
    vmem = pl.BlockSpec(memory_space=pltpu.VMEM)
    hbm = pl.BlockSpec(memory_space=pl.ANY)
    dma = pltpu.SemaphoreType.DMA
    others = max(nchip - 1, 1)
    return pl.pallas_call(
        functools.partial(front_kernel, n_seq, n_tp),
        out_shape=[jax.ShapeDtypeStruct((tokens, width), BF16)] * 2
        + [jax.ShapeDtypeStruct((tokens, ffw), BF16)] * 3
        + [jax.ShapeDtypeStruct((tokens, width), F32)],
        in_specs=[vmem, vmem, hbm, hbm, hbm],
        out_specs=[vmem] * 6,
        scratch_shapes=[
            pltpu.VMEM((2, nz, 2, rows, width), BF16),
            pltpu.VMEM(wg.shape, BF16),
            pltpu.VMEM(wu.shape, BF16),
            pltpu.VMEM(wd.shape, BF16),
            pltpu.VMEM((3, nchip, 2, share, ffw), F32),
            pltpu.VMEM((3, nchip, share, ffw), F32),
            pltpu.VMEM((3, share, ffw), F32),
            pltpu.VMEM((3, others, share, ffw), BF16),
            pltpu.VMEM((3, others, share, ffw), BF16),
            pltpu.VMEM((3, nchip, 2, share, ffw), BF16),
            dma((3,)),
            dma((2, nz)), dma((2, nz)), dma((2, nz)), dma((2, nz)),
            dma((3,)), dma((3,)),
            dma((3, nchip)), dma((3, nchip)),
            dma((3, nchip)), dma((3, nchip)), dma((3, nchip)), dma((3, nchip)),
        ],
        compiler_params=pltpu.CompilerParams(
            collective_id=0, has_side_effects=True, vmem_limit_bytes=48 * 1024 * 1024
        ),
        cost_estimate=pl.CostEstimate(
            flops=10 * tokens * width * ffw, bytes_accessed=6 * width * ffw, transcendentals=0
        ),
    )(x, dy, wg, wu, wd)


def weight_kernel(pairs, *refs):
    lefts, rights, outs = refs[:pairs], refs[pairs : 2 * pairs], refs[2 * pairs :]
    for left, right, out in zip(lefts, rights, outs):
        turn = left[...].astype(F32).T.astype(BF16)
        out[...] = jnp.dot(turn, right[...], preferred_element_type=F32)


def weight_grads(left, rights):
    tokens, rows = left.shape
    pairs = len(rights)
    steps = pl.cdiv(rows, ROWS)
    return pl.pallas_call(
        functools.partial(weight_kernel, pairs),
        grid=(steps,),
        out_shape=[jax.ShapeDtypeStruct((rows, right.shape[1]), F32) for right in rights],
        in_specs=[pl.BlockSpec((tokens, ROWS), lambda i: (0, i))] * pairs
        + [pl.BlockSpec(right.shape, lambda i: (0, 0)) for right in rights],
        out_specs=[pl.BlockSpec((ROWS, right.shape[1]), lambda i: (i, 0)) for right in rights],
        cost_estimate=pl.CostEstimate(
            flops=2 * tokens * rows * sum(right.shape[1] for right in rights),
            bytes_accessed=4 * rows * sum(right.shape[1] for right in rights),
            transcendentals=0,
        ),
    )(*([left] * pairs), *rights)


def scatter_sum(n_seq, partial):
    nz = n_seq // 2
    seq = lax.axis_index("seq")
    z, y = seq // 2, lax.rem(seq, 2)
    rows = partial.shape[0] // n_seq
    pieces = partial.reshape(nz, 2, rows, partial.shape[1])
    away = lax.dynamic_index_in_dim(pieces, 1 - y, 1, keepdims=False)
    kept = lax.dynamic_index_in_dim(pieces, y, 1, keepdims=False)
    summed = kept + lax.ppermute(away, "seq", [(i, i ^ 1) for i in range(n_seq)])
    result = lax.dynamic_index_in_dim(summed, z, 0, keepdims=False)
    for k in range(1, nz):
        send = lax.dynamic_index_in_dim(summed, lax.rem(z + k, nz), 0, keepdims=False)
        result = result + lax.ppermute(
            send, "seq", [(i, (i + 2 * k) % n_seq) for i in range(n_seq)]
        )
    return result


def solution(mesh):
    n_seq, n_tp = mesh.shape["seq"], mesh.shape["tp"]

    def per_device(inputs, out_grad, gate_weight, up_weight, down_weight):
        blocks, rows, width = inputs.shape
        x, dy, hidden, gate_unit, up_unit, partial = front(
            n_seq, n_tp,
            inputs.reshape(blocks * rows, width), out_grad.reshape(blocks * rows, width),
            gate_weight, up_weight, down_weight,
        )
        gate_grad, up_grad = weight_grads(x, (gate_unit, up_unit))
        (down_grad,) = weight_grads(hidden, (dy,))
        input_grad = scatter_sum(n_seq, partial).astype(BF16).reshape(inputs.shape)
        return input_grad, gate_grad, up_grad, down_grad

    return jax.shard_map(
        per_device,
        mesh=mesh,
        in_specs=(
            P(None, "seq", "tp"),
            P(None, "seq", "tp"),
            P("tp", "seq"),
            P("tp", "seq"),
            P("seq", "tp"),
        ),
        out_specs=(P(None, "seq", "tp"), P("tp", "seq"), P("tp", "seq"), P("seq", "tp")),
        check_vma=False,
    )
```

time: 336 us -> 138 us (0.41)
  blocking collectives: 192 us -> 0 us
  matrix products: 82.2 us -> 0 us
  Pallas kernels: 0 us -> 66.2 us
  local copies, waits for them, and re-layouts: 2.53 us -> 55.9 us
  waiting for transfers between devices: 40.2 us -> 6.45 us
  between operations: 15.5 us -> 0.73 us
  starting transfers between devices: 0.04 us -> 6.52 us
    all_gather x8 -> x0, blocking collectives: 149 us -> none  [the longest x2 63.7 us: per_device(): whole_grad = lax.all_gather(out_grad[index], 'seq', axis=0, tiled=True)]
    dot_general x16 -> x0, matrix products: 82.2 us -> none  [the longest x2 21 us: per_device(): lax.dot_general(whole_in, front_unit_gate, contract_first, preferred_elem...]
    pallas_call x0 -> x3, Pallas kernels: none -> 66.2 us  [the longest x1 39.4 us: front(): pl.pallas_call(functools.partial(front_kernel, n_seq, n_tp), out_shape=[j...]
    unnamed x46 -> x18, local copies, waits for them, and re-layouts: 1.59 us -> 55.1 us
    unnamed x1 -> x0, blocking collectives: 43.3 us -> none
    psum x1 -> x0, waiting for transfers between devices: 40.2 us -> none  [per_device(): gate, up_proj = lax.psum((gate_part, up_part), 'tp')]
    ppermute x0 -> x4, starting transfers between devices: none -> 6.52 us  [the longest x3 4.09 us: scatter_sum(): lax.ppermute(send, 'seq', [(i, (i + 2 * k) % n_seq) for i in range(n_seq)])]
    ppermute x0 -> x4, waiting for transfers between devices: none -> 6.45 us  [the longest x1 6.44 us: scatter_sum(): lax.ppermute(away, 'seq', [(i, i ^ 1) for i in range(n_seq)])]
  transfers between devices with their start and end apart: 1 -> 4, of which waited for: 1 -> 1; matrix products, arithmetic and copies ran while one was open for 0% -> 23% of each run, Pallas kernels for 0% -> 20%
where the time goes in v1:
time: 138 us; the launch traced here: 136 us
  Pallas kernels  66.2 us (48%)
  local copies, waits for them, and re-layouts  55.9 us (41%)
  starting transfers between devices  6.52 us (5%)
  waiting for transfers between devices  6.45 us (5%)
    unnamed x18, local copies, waits for them, and re-layouts  55.1 us
    pallas_call x1, Pallas kernels, front(): pl.pallas_call(functools.partial(front_kernel, n_seq, n_tp), out_shape=[j...  39.4 us
    pallas_call x2, Pallas kernels, weight_grads(): pl.pallas_call(functools.partial(weight_kernel, pairs), grid=(steps,), ou...  26.8 us
    ppermute x1, waiting for transfers between devices, scatter_sum(): lax.ppermute(away, 'seq', [(i, i ^ 1) for i in range(n_seq)])  6.44 us
    ppermute x3, starting transfers between devices, scatter_sum(): lax.ppermute(send, 'seq', [(i, (i + 2 * k) % n_seq) for i in range(n_seq)])  4.09 us
  transfers between devices with their start and end apart: 4, of which 1 were waited for; matrix products, arithmetic and copies ran while one was open for 23% of the time, Pallas kernels for 20%

profile of v1, /device:TPU:0, one launch (start us, length us, event | category | flops | bytes accessed | tf_op | source)
XLA Modules:
  0.0 135.8 jit_solution(12731825022291185035)
XLA Ops:
  0.6 0.0 copy-start.5
  0.6 0.0 copy-start.6
  0.7 10.3 %copy.10.wu_hbm = bf16[2048,1856]{1,0:T(8,128)(2,1)} copy(bf16[2048,1856]{0,1:T(8,128)(2,1)} %param.8) | data formatting | bytes 15204352 | tf_op args[3]
  11.0 10.3 %copy.9.wg_hbm = bf16[2048,1856]{1,0:T(8,128)(2,1)} copy(bf16[2048,1856]{0,1:T(8,128)(2,1)} %param.7) | data formatting | bytes 15204352 | tf_op args[2]
  21.3 0.0 copy-done.5
  21.3 0.0 copy-done.6
  21.3 39.4 %shard_map.84 = (bf16[64,2048]{1,0:T(8,128)(2,1)S(1)}, bf16[64,2048]{1,0:T(8,128)(2,1)S(1)}, bf16[64,1856]{1,0:T(8,128)(2,1)S(1)}, bf16[64,1856]{1,0:T(8,128)(2,...) custom-call(bf16[8,2048]{1,0:T(8,128)(2,1)S(1)} %reshape.20.x_ref, bf16[8,2048]{1,0:T(8,128)(2,1)S(1)} %reshape.21.dy_ref, ...), custom_call_target="tpu_custom_call" | custom-call | flops 2432696320 | bytes 22806528 | tf_op jit(solution)/shard_map/pallas_call | solution.py:226
  60.7 0.0 copy-start
  60.7 0.7 copy-done
  61.4 0.0 copy-start.1
  61.4 0.7 copy-done.1
  62.1 0.0 copy-start.2
  62.1 0.7 copy-done.2
  62.8 0.0 copy-start.3
  62.8 0.7 copy-done.3
  63.5 0.0 copy-start.4
  63.5 0.7 copy-done.4
  64.2 2.4 %collective-permute-start = (f32[4,8,2048]{2,1,0:T(8,128)S(1)}, f32[4,8,2048]{2,1,0:T(8,128)S(1)}, u32[]{:S(2)}, u32[]{:S(2)}) collective-permute-start(f32[4,8,2048]{2,1,0:T(8,128)S(1)} %dynamic-slice_bitcast_fusion), channel_id=1, source_target_pairs={{0,4},{4,0},{8,12},{12,8},{16,20},{20,16},{24,28},{28,24},{1,5},{5... | collective-permute-start | bytes 786440 | tf_op jit(solution)/shard_map/ppermute | solution.py:293
  66.7 6.4 %collective-permute-done = f32[4,8,2048]{2,1,0:T(8,128)S(1)} collective-permute-done((f32[4,8,2048]{2,1,0:T(8,128)S(1)}, f32[4,8,2048]{2,1,0:T(8,128)S(1)}, u32[]{:S(2)}, u32[]{:S(2)}) %collective-permute-start) | collective-permute-done | bytes 262176 | tf_op jit(solution)/shard_map/ppermute | solution.py:293
  73.2 1.2 collective-permute-start.1
  74.4 2.1 %collective-permute-start.2 = (f32[8,2048]{1,0:T(8,128)S(1)}, f32[8,2048]{1,0:T(8,128)S(1)}, u32[]{:S(2)}, u32[]{:S(2)}) collective-permute-start(f32[8,2048]{1,0:T(8,128)S(1)} %get-tuple-element.26), channel_id=1, source_target_pairs={{0,16},{4,20},{8,24},{12,28},{16,0},{20,4},{24,8},{28,12},{1,17},{... | collective-permute-start | bytes 196616 | tf_op jit(solution)/shard_map/ppermute | solution.py:297
  76.5 0.8 collective-permute-start.3
  77.3 15.2 %shard_map.85 = (f32[2048,1856]{1,0:T(8,128)}, f32[2048,1856]{1,0:T(8,128)}) custom-call(bf16[64,2048]{1,0:T(8,128)(2,1)} %copy-done.2, bf16[64,2048]{1,0:T(8,128)(2,1)} %copy-done.2, bf16[64,1856]{1,0:T(8,128)(2,1)} %copy-done.3, bf16[64,1856]{1,0:T(8,128)(2,1)} %copy-done.4), custom_call_target="tpu_custom_call" | custom-call | flops 973078528 | bytes 30408704 | tf_op jit(solution)/shard_map/pallas_call | solution.py:270
  92.5 15.5 %copy.11 = f32[2048,1856]{0,1:T(8,128)} copy(f32[2048,1856]{1,0:T(8,128)} %get-tuple-element.21) | data formatting | bytes 30408704
  108.0 15.5 %copy.12 = f32[2048,1856]{0,1:T(8,128)} copy(f32[2048,1856]{1,0:T(8,128)} %get-tuple-element.22) | data formatting | bytes 30408704
  123.5 11.6 %shard_map.86 = f32[1856,2048]{1,0:T(8,128)} custom-call(bf16[64,1856]{1,0:T(8,128)(2,1)} %copy-done.1, bf16[64,2048]{1,0:T(8,128)(2,1)} %copy-done), custom_call_target="tpu_custom_call" | custom-call | flops 486539264 | bytes 15204352 | tf_op jit(solution)/shard_map/pallas_call | solution.py:270
  135.1 0.0 collective-permute-done.1
  135.1 0.0 collective-permute-done.2
  135.2 0.0 collective-permute-done.3
  135.2 0.6 reshape.23
  (6 shorter events, 0.1 us)
Async XLA Ops:
  0.6 20.6 %copy-start.5 = (bf16[2,4,2048]{2,1,0:T(4,128)(2,1)S(1)}, bf16[2,4,2048]{2,1,0:T(4,128)(2,1)}, u32[]{:S(2)}) copy-start(bf16[2,4,2048]{2,1,0:T(4,128)(2,1)} %param.5) | copy-start | bytes 98308
  0.6 20.6 %copy-start.6 = (bf16[2,4,2048]{2,1,0:T(4,128)(2,1)S(1)}, bf16[2,4,2048]{2,1,0:T(4,128)(2,1)}, u32[]{:S(2)}) copy-start(bf16[2,4,2048]{2,1,0:T(4,128)(2,1)} %param.6) | copy-start | bytes 98308
  60.7 0.7 copy-start
  61.4 0.7 copy-start.1
  62.1 0.7 copy-start.2
  62.8 0.7 copy-start.3
  63.5 0.7 copy-start.4
  64.2 8.9 %collective-permute-start = (f32[4,8,2048]{2,1,0:T(8,128)S(1)}, f32[4,8,2048]{2,1,0:T(8,128)S(1)}, u32[]{:S(2)}, u32[]{:S(2)}) collective-permute-start(f32[4,8,2048]{2,1,0:T(8,128)S(1)} %dynamic-slice_bitcast_fusion), channel_id=1, source_target_pairs={{0,4},{4,0},{8,12},{12,8},{16,20},{20,16},{24,28},{28,24},{1,5},{5... | collective-permute-start | bytes 786440 | tf_op jit(solution)/shard_map/ppermute | solution.py:293
  73.2 62.0 %collective-permute-start.1 = (f32[8,2048]{1,0:T(8,128)S(1)}, f32[8,2048]{1,0:T(8,128)S(1)}, u32[]{:S(2)}, u32[]{:S(2)}) collective-permute-start(f32[8,2048]{1,0:T(8,128)S(1)} %get-tuple-element.24), channel_id=1, source_target_pairs={{0,8},{4,12},{8,16},{12,20},{16,24},{20,28},{24,0},{28,4},{1,9},{5... | collective-permute-start | bytes 196616 | tf_op jit(solution)/shard_map/ppermute | solution.py:297
  74.4 60.8 %collective-permute-start.2 = (f32[8,2048]{1,0:T(8,128)S(1)}, f32[8,2048]{1,0:T(8,128)S(1)}, u32[]{:S(2)}, u32[]{:S(2)}) collective-permute-start(f32[8,2048]{1,0:T(8,128)S(1)} %get-tuple-element.26), channel_id=1, source_target_pairs={{0,16},{4,20},{8,24},{12,28},{16,0},{20,4},{24,8},{28,12},{1,17},{... | collective-permute-start | bytes 196616 | tf_op jit(solution)/shard_map/ppermute | solution.py:297
  76.5 58.7 %collective-permute-start.3 = (f32[8,2048]{1,0:T(8,128)S(1)}, f32[8,2048]{1,0:T(8,128)S(1)}, u32[]{:S(2)}, u32[]{:S(2)}) collective-permute-start(f32[8,2048]{1,0:T(8,128)S(1)} %get-tuple-element.25), channel_id=1, source_target_pairs={{0,24},{4,28},{8,0},{12,4},{16,8},{20,12},{24,16},{28,20},{1,25},{... | collective-permute-start | bytes 196616 | tf_op jit(solution)/shard_map/ppermute | solution.py:297

commit v2 on v1

--- a/solution.py
+++ b/solution.py
@@ -12,7 +12,6 @@
 BF16 = jnp.bfloat16
 NT = (((1,), (1,)), ((), ()))
 TILE = 256
-ROWS = 128
 
 
 def tiles_of(size, tile, body):
@@ -36,7 +35,8 @@
     nz, nchip = n_seq // 2, n_tp // 2
     z, y = seq // 2, lax.rem(seq, 2)
     chip, core = tp // 2, lax.rem(tp, 2)
-    tokens, ffw = hid_out.shape
+    tokens = hid_out.shape[0]
+    ffw = wg_hbm.shape[0]
     share = tokens // n_tp
     at_y = {"seq": z * 2 + (1 - y)}
     at_core = {"tp": chip * 2 + (1 - core)}
@@ -112,12 +112,9 @@
         for q in range(3)
     ]
 
-    def product(q, out, w, last):
+    def product(q, out, w):
         def body(start, width):
-            if last:
-                val = lax.dot_general(out[...], w[pl.ds(start, width), :], NT, preferred_element_type=F32)
-            else:
-                val = jnp.dot(out[...], w[:, pl.ds(start, width)], preferred_element_type=F32)
+            val = lax.dot_general(out[...], w[pl.ds(start, width), :], NT, preferred_element_type=F32)
             part[q, :, :, :, pl.ds(start, width)] = val.reshape(nchip, 2, share, width)
 
         tiles_of(ffw, TILE, body)
@@ -133,15 +130,15 @@
     forward(0)
     arrive(0, x_out)
     loads[0].wait()
-    product(0, x_out, wg, False)
+    product(0, x_out, wg)
     forward(1)
     loads[1].wait()
-    product(1, x_out, wu, False)
+    product(1, x_out, wu)
     reduce_chip(0)
     reduce_chip(1)
     arrive(1, dy_out)
     loads[2].wait()
-    product(2, dy_out, wd, True)
+    product(2, dy_out, wd)
     reduce_chip(2)
     for q in range(3):
         for k in range(1, nchip):
@@ -185,11 +182,14 @@
     def collect(q):
         for k in range(nchip):
             f_copies[q][k].wait_recv()
-        outs[q][...] = acts[q].reshape(tokens, ffw)
+        if outs[q].shape[1] > ffw:
+            start = ffw // 128 * 128
+            outs[q][:, start:] = jnp.zeros((tokens, outs[q].shape[1] - start), BF16)
+        outs[q][:, :ffw] = acts[q].reshape(tokens, ffw)
 
     def back(q, w):
         def body(start, width):
-            val = lax.dot_general(outs[q][...], w[pl.ds(start, width), :], NT, preferred_element_type=F32)
+            val = jnp.dot(outs[q][:, :ffw], w[:, pl.ds(start, width)], preferred_element_type=F32)
             if q:
                 val = val + ig_out[:, pl.ds(start, width)]
             ig_out[:, pl.ds(start, width)] = val
@@ -215,7 +215,8 @@
 
 def front(n_seq, n_tp, x, dy, wg, wu, wd):
     rows, width = x.shape
-    ffw = wg.shape[1]
+    ffw = wg.shape[0]
+    padded = pl.cdiv(ffw, TILE) * TILE
     tokens = rows * n_seq
     nz, nchip = n_seq // 2, n_tp // 2
     share = tokens // n_tp
@@ -226,7 +227,7 @@
     return pl.pallas_call(
         functools.partial(front_kernel, n_seq, n_tp),
         out_shape=[jax.ShapeDtypeStruct((tokens, width), BF16)] * 2
-        + [jax.ShapeDtypeStruct((tokens, ffw), BF16)] * 3
+        + [jax.ShapeDtypeStruct((tokens, padded), BF16)] * 3
         + [jax.ShapeDtypeStruct((tokens, width), F32)],
         in_specs=[vmem, vmem, hbm, hbm, hbm],
         out_specs=[vmem] * 6,
@@ -257,32 +258,31 @@
 
 
 def weight_kernel(pairs, *refs):
-    lefts, rights, outs = refs[:pairs], refs[pairs : 2 * pairs], refs[2 * pairs :]
-    for left, right, out in zip(lefts, rights, outs):
-        turn = left[...].astype(F32).T.astype(BF16)
-        out[...] = jnp.dot(turn, right[...], preferred_element_type=F32)
-
-
-def weight_grads(left, rights):
-    tokens, rows = left.shape
-    pairs = len(rights)
-    steps = pl.cdiv(rows, ROWS)
+    lefts, right, outs = refs[:pairs], refs[pairs], refs[pairs + 1 :]
+    columns = pl.ds(pl.multiple_of(pl.program_id(0) * TILE, TILE), TILE)
+    for left, out in zip(lefts, outs):
+        turned = left[:, columns].astype(F32).T.astype(BF16)
+        out[...] = jnp.dot(turned, right[...], preferred_element_type=F32)
+
+
+def weight_grads(rows, lefts, right):
+    tokens, width = right.shape
+    pairs = len(lefts)
     return pl.pallas_call(
         functools.partial(weight_kernel, pairs),
-        grid=(steps,),
-        out_shape=[jax.ShapeDtypeStruct((rows, right.shape[1]), F32) for right in rights],
-        in_specs=[pl.BlockSpec((tokens, ROWS), lambda i: (0, i))] * pairs
-        + [pl.BlockSpec(right.shape, lambda i: (0, 0)) for right in rights],
-        out_specs=[pl.BlockSpec((ROWS, right.shape[1]), lambda i: (i, 0)) for right in rights],
+        grid=(pl.cdiv(rows, TILE),),
+        out_shape=[jax.ShapeDtypeStruct((rows, width), F32)] * pairs,
+        in_specs=[pl.BlockSpec(memory_space=pltpu.VMEM)] * (pairs + 1),
+        out_specs=[pl.BlockSpec((TILE, width), lambda i: (i, 0))] * pairs,
         cost_estimate=pl.CostEstimate(
-            flops=2 * tokens * rows * sum(right.shape[1] for right in rights),
-            bytes_accessed=4 * rows * sum(right.shape[1] for right in rights),
+            flops=2 * pairs * tokens * rows * width,
+            bytes_accessed=4 * pairs * rows * width,
             transcendentals=0,
         ),
-    )(*([left] * pairs), *rights)
-
-
-def scatter_sum(n_seq, partial):
+    )(*lefts, right)
+
+
+def scatter_sum(n_seq, partial, cover):
     nz = n_seq // 2
     seq = lax.axis_index("seq")
     z, y = seq // 2, lax.rem(seq, 2)
@@ -290,14 +290,16 @@
     pieces = partial.reshape(nz, 2, rows, partial.shape[1])
     away = lax.dynamic_index_in_dim(pieces, 1 - y, 1, keepdims=False)
     kept = lax.dynamic_index_in_dim(pieces, y, 1, keepdims=False)
-    summed = kept + lax.ppermute(away, "seq", [(i, i ^ 1) for i in range(n_seq)])
+    arrived = lax.ppermute(away, "seq", [(i, i ^ 1) for i in range(n_seq)])
+    kept, *cover = lax.optimization_barrier((kept, *cover))
+    summed = kept + arrived
     result = lax.dynamic_index_in_dim(summed, z, 0, keepdims=False)
     for k in range(1, nz):
         send = lax.dynamic_index_in_dim(summed, lax.rem(z + k, nz), 0, keepdims=False)
         result = result + lax.ppermute(
             send, "seq", [(i, (i + 2 * k) % n_seq) for i in range(n_seq)]
         )
-    return result
+    return result, cover
 
 
 def solution(mesh):
@@ -308,12 +310,13 @@
         x, dy, hidden, gate_unit, up_unit, partial = front(
             n_seq, n_tp,
             inputs.reshape(blocks * rows, width), out_grad.reshape(blocks * rows, width),
-            gate_weight, up_weight, down_weight,
+            gate_weight.T, up_weight.T, down_weight,
         )
-        gate_grad, up_grad = weight_grads(x, (gate_unit, up_unit))
-        (down_grad,) = weight_grads(hidden, (dy,))
-        input_grad = scatter_sum(n_seq, partial).astype(BF16).reshape(inputs.shape)
-        return input_grad, gate_grad, up_grad, down_grad
+        hidden_units = down_weight.shape[0]
+        cover = weight_grads(hidden_units, (gate_unit, up_unit), x)
+        total, (gate_grad, up_grad) = scatter_sum(n_seq, partial, cover)
+        (down_grad,) = weight_grads(hidden_units, (hidden,), dy)
+        return total.astype(BF16).reshape(inputs.shape), gate_grad.T, up_grad.T, down_grad
 
     return jax.shard_map(
         per_device,

time: 138 us -> 69.9 us (0.51); the launches traced: 136 us -> 69.7 us
  local copies, waits for them, and re-layouts: 55.9 us -> 3.83 us
  waiting for transfers between devices: 6.45 us -> 0.01 us
  Pallas kernels: 66.2 us -> 59.9 us
  starting transfers between devices: 6.52 us -> 5.13 us
    unnamed x18 -> x10, local copies, waits for them, and re-layouts: 55.1 us -> 1.58 us
    ppermute x1, waiting for transfers between devices: 6.44 us -> 0.01 us  [scatter_sum(): arrived = lax.ppermute(away, 'seq', [(i, i ^ 1) for i in range(n_seq)])]
    pallas_call x2, Pallas kernels: 26.8 us -> 20.6 us  [weight_grads(): pl.pallas_call(functools.partial(weight_kernel, pairs), grid=(pl.cdiv(row...]
    ppermute x1, starting transfers between devices: 2.42 us -> 0.66 us  [scatter_sum(): arrived = lax.ppermute(away, 'seq', [(i, i ^ 1) for i in range(n_seq)])]
  transfers between devices with their start and end apart: 4 -> 4, of which waited for: 1 -> 0; matrix products, arithmetic and copies ran while one was open for 23% -> 0% of each run, Pallas kernels for 20% -> 30%
where the time goes in v2:
time: 69.9 us; the launch traced here: 69.7 us
  Pallas kernels  59.9 us (86%)
  starting transfers between devices  5.13 us (7%)
  local copies, waits for them, and re-layouts  3.83 us (5%)
  between operations  0.7 us (1%)
    pallas_call x1, Pallas kernels, front(): pl.pallas_call(functools.partial(front_kernel, n_seq, n_tp), out_shape=[j...  39.3 us
    pallas_call x2, Pallas kernels, weight_grads(): pl.pallas_call(functools.partial(weight_kernel, pairs), grid=(pl.cdiv(row...  20.6 us
    ppermute x3, starting transfers between devices, scatter_sum(): lax.ppermute(send, 'seq', [(i, (i + 2 * k) % n_seq) for i in range(n_seq)])  4.47 us
    unnamed x10, local copies, waits for them, and re-layouts  1.58 us
  transfers between devices with their start and end apart: 4, of which 0 were waited for; matrix products, arithmetic and copies ran while one was open for 0% of the time, Pallas kernels for 30%

profile of v2, /device:TPU:0, one launch (start us, length us, event | category | flops | bytes accessed | tf_op | source)
XLA Modules:
  0.0 69.7 jit_solution(12596748421899042372)
XLA Ops:
  0.6 0.8 %reshape.20.x_ref = bf16[8,2048]{1,0:T(8,128)(2,1)S(1)} reshape(bf16[2,4,2048]{2,1,0:T(4,128)(2,1)} %param.5) | data formatting | bytes 65536 | tf_op jit(solution)/shard_map/reshape | solution.py:312
  1.4 0.8 %reshape.21.dy_ref = bf16[8,2048]{1,0:T(8,128)(2,1)S(1)} reshape(bf16[2,4,2048]{2,1,0:T(4,128)(2,1)} %param.6) | data formatting | bytes 65536 | tf_op jit(solution)/shard_map/reshape | solution.py:312
  2.2 39.3 %shard_map.84 = (bf16[64,2048]{1,0:T(8,128)(2,1)S(1)}, bf16[64,2048]{1,0:T(8,128)(2,1)S(1)}, bf16[64,2048]{1,0:T(8,128)(2,1)S(1)}, bf16[64,2048]{1,0:T(8,128)(2,...) custom-call(bf16[8,2048]{1,0:T(8,128)(2,1)S(1)} %reshape.20.x_ref, bf16[8,2048]{1,0:T(8,128)(2,1)S(1)} %reshape.21.dy_ref, ...), custom_call_target="tpu_custom_call" | custom-call | flops 2432696320 | bytes 22806528 | tf_op jit(solution)/shard_map/pallas_call | solution.py:227
  41.5 0.0 copy-start.4
  41.5 0.7 copy-done.4
  42.2 0.0 copy-start
  42.2 0.0 copy-start.1
  42.2 0.0 copy-start.2
  42.2 0.0 copy-start.3
  42.2 0.7 copy-done
  42.9 0.1 copy-done.1
  43.0 0.1 copy-done.2
  43.1 0.1 copy-done.3
  43.1 0.7 collective-permute-start
  43.8 12.3 %shard_map.85 = (f32[1856,2048]{1,0:T(8,128)}, f32[1856,2048]{1,0:T(8,128)}) custom-call(bf16[64,2048]{1,0:T(8,128)(2,1)} %copy-done.3, bf16[64,2048]{1,0:T(8,128)(2,1)} %copy-done.4, bf16[64,2048]{1,0:T(8,128)(2,1)} %copy-done.2), custom_call_target="tpu_custom_call" | custom-call | flops 973078528 | bytes 30408704 | tf_op jit(solution)/shard_map/pallas_call | solution.py:271
  56.1 0.0 collective-permute-done
  56.1 2.0 %collective-permute-start.1 = (f32[8,2048]{1,0:T(8,128)S(1)}, f32[8,2048]{1,0:T(8,128)S(1)}, u32[]{:S(2)}, u32[]{:S(2)}) collective-permute-start(f32[8,2048]{1,0:T(8,128)S(1)} %get-tuple-element.28), channel_id=1, source_target_pairs={{0,8},{4,12},{8,16},{12,20},{16,24},{20,28},{24,0},{28,4},{1,9},{5... | collective-permute-start | bytes 196616 | tf_op jit(solution)/shard_map/ppermute | solution.py:299
  58.2 1.3 %collective-permute-start.2 = (f32[8,2048]{1,0:T(8,128)S(1)}, f32[8,2048]{1,0:T(8,128)S(1)}, u32[]{:S(2)}, u32[]{:S(2)}) collective-permute-start(f32[8,2048]{1,0:T(8,128)S(1)} %get-tuple-element.30), channel_id=1, source_target_pairs={{0,16},{4,20},{8,24},{12,28},{16,0},{20,4},{24,8},{28,12},{1,17},{... | collective-permute-start | bytes 196616 | tf_op jit(solution)/shard_map/ppermute | solution.py:299
  59.5 1.1 %collective-permute-start.3 = (f32[8,2048]{1,0:T(8,128)S(1)}, f32[8,2048]{1,0:T(8,128)S(1)}, u32[]{:S(2)}, u32[]{:S(2)}) collective-permute-start(f32[8,2048]{1,0:T(8,128)S(1)} %get-tuple-element.29), channel_id=1, source_target_pairs={{0,24},{4,28},{8,0},{12,4},{16,8},{20,12},{24,16},{28,20},{1,25},{... | collective-permute-start | bytes 196616 | tf_op jit(solution)/shard_map/ppermute | solution.py:299
  60.6 8.4 %shard_map.86 = f32[1856,2048]{1,0:T(8,128)} custom-call(bf16[64,2048]{1,0:T(8,128)(2,1)} %copy-done.1, bf16[64,2048]{1,0:T(8,128)(2,1)} %copy-done), custom_call_target="tpu_custom_call" | custom-call | flops 486539264 | bytes 15204352 | tf_op jit(solution)/shard_map/pallas_call | solution.py:271
  69.0 0.0 collective-permute-done.1
  69.0 0.0 collective-permute-done.2
  69.0 0.0 collective-permute-done.3
  69.0 0.6 reshape.23
  (4 shorter events, 0.1 us)
Async XLA Ops:
  41.5 0.7 copy-start.4
  42.2 0.7 %copy-start = (bf16[64,2048]{1,0:T(8,128)(2,1)}, bf16[64,2048]{1,0:T(8,128)(2,1)S(1)}, u32[]{:S(2)}) copy-start(bf16[64,2048]{1,0:T(8,128)(2,1)S(1)} %get-tuple-element.25.refs_1_) | copy-start | bytes 786436
  42.2 0.8 %copy-start.1 = (bf16[64,2048]{1,0:T(8,128)(2,1)}, bf16[64,2048]{1,0:T(8,128)(2,1)S(1)}, u32[]{:S(2)}) copy-start(bf16[64,2048]{1,0:T(8,128)(2,1)S(1)} %get-tuple-element.24.refs_0_) | copy-start | bytes 786436
  42.2 0.9 %copy-start.2 = (bf16[64,2048]{1,0:T(8,128)(2,1)}, bf16[64,2048]{1,0:T(8,128)(2,1)S(1)}, u32[]{:S(2)}) copy-start(bf16[64,2048]{1,0:T(8,128)(2,1)S(1)} %get-tuple-element.18.refs_2_) | copy-start | bytes 786436
  42.2 1.0 %copy-start.3 = (bf16[64,2048]{1,0:T(8,128)(2,1)}, bf16[64,2048]{1,0:T(8,128)(2,1)S(1)}, u32[]{:S(2)}) copy-start(bf16[64,2048]{1,0:T(8,128)(2,1)S(1)} %get-tuple-element.16.refs_0_) | copy-start | bytes 786436
  43.1 12.9 %collective-permute-start = (f32[4,8,2048]{2,1,0:T(8,128)S(1)}, f32[4,8,2048]{2,1,0:T(8,128)S(1)}, u32[]{:S(2)}, u32[]{:S(2)}) collective-permute-start(f32[4,8,2048]{2,1,0:T(8,128)S(1)} %get-tuple-element.26), channel_id=1, source_target_pairs={{0,4},{4,0},{8,12},{12,8},{16,20},{20,16},{24,28},{28,24},{1,5},{5... | collective-permute-start | bytes 786440 | tf_op jit(solution)/shard_map/ppermute | solution.py:293
  56.1 12.8 %collective-permute-start.1 = (f32[8,2048]{1,0:T(8,128)S(1)}, f32[8,2048]{1,0:T(8,128)S(1)}, u32[]{:S(2)}, u32[]{:S(2)}) collective-permute-start(f32[8,2048]{1,0:T(8,128)S(1)} %get-tuple-element.28), channel_id=1, source_target_pairs={{0,8},{4,12},{8,16},{12,20},{16,24},{20,28},{24,0},{28,4},{1,9},{5... | collective-permute-start | bytes 196616 | tf_op jit(solution)/shard_map/ppermute | solution.py:299
  58.2 10.8 %collective-permute-start.2 = (f32[8,2048]{1,0:T(8,128)S(1)}, f32[8,2048]{1,0:T(8,128)S(1)}, u32[]{:S(2)}, u32[]{:S(2)}) collective-permute-start(f32[8,2048]{1,0:T(8,128)S(1)} %get-tuple-element.30), channel_id=1, source_target_pairs={{0,16},{4,20},{8,24},{12,28},{16,0},{20,4},{24,8},{28,12},{1,17},{... | collective-permute-start | bytes 196616 | tf_op jit(solution)/shard_map/ppermute | solution.py:299
  59.5 9.5 %collective-permute-start.3 = (f32[8,2048]{1,0:T(8,128)S(1)}, f32[8,2048]{1,0:T(8,128)S(1)}, u32[]{:S(2)}, u32[]{:S(2)}) collective-permute-start(f32[8,2048]{1,0:T(8,128)S(1)} %get-tuple-element.29), channel_id=1, source_target_pairs={{0,24},{4,28},{8,0},{12,4},{16,8},{20,12},{24,16},{28,20},{1,25},{... | collective-permute-start | bytes 196616 | tf_op jit(solution)/shard_map/ppermute | solution.py:299
